TPU v7x, 32 devices: a whole 2x2x4 slice. The times are simulated.
32 devices in a mesh: kvp: 16 (over z, y, x), tp: 2 (over core).
Axes of the slice: x: 2, y: 2, z: 4, core: 2. Of those that a mesh axis runs over, the one named last changes fastest.
Arguments:
- queries: bfloat16 [8, 8192], P(None, 'tp'), may hold values from -12 to 12
- key_pool: bfloat16 [512, 64, 1024], P('kvp', None, 'tp'), may hold values from -5 to 5
- value_pool: bfloat16 [512, 64, 1024], P('kvp', None, 'tp'), may hold values from -5 to 5
- block_table: int32 [16, 32], P('kvp'), may hold values from 0 to 31, each once within a row
- lengths: int32 [8], replicated, may hold values from 1 to 4096, 20480 in all
- residual_in: float32 [8, 8192], P(None, 'kvp'), may hold values from -12 to 12
- out_weight: bfloat16 [8192, 8192], P('tp', 'kvp'), may hold values from -0.0625 to 0.0625
- norm_gain: bfloat16 [8192], P('kvp'), may hold values from 0.25 to 1.75
- gate_weight: bfloat16 [8192, 28672], P('kvp', 'tp'), may hold values from -0.0625 to 0.0625
- up_weight: bfloat16 [8192, 28672], P('kvp', 'tp'), may hold values from -0.0625 to 0.0625
- down_weight: bfloat16 [28672, 8192], P('tp', 'kvp'), may hold values from -0.03125 to 0.03125
Outputs:
- attended: bfloat16 [8, 8192], P(None, 'tp')
- layer_out: float32 [8, 8192], P(None, 'kvp')
Inputs may be any that keep to these rules, and one draw needn't show every extreme that they name: Row s is a permutation of 0 to 31; the page of request b's block j in KV shard s is s * 32 + block_table[s, b * 4 + j]. The lengths sum to 20480 and the longest is exactly 4096.
All inputs are finite; a program needn't handle non-finite values.
Results may differ from a plain program's by a relative error of at most 0.0056.
Values may be sent and summed in bfloat16 or wider, within the bound.
A program may use at most 128 MiB of HBM per device.

v0:
```python
import jax
import jax.numpy as jnp
from jax import lax
from jax.sharding import PartitionSpec as P

D = 8192
HD = 128


def merged(part, axis, combine):
    gathered = jax.tree.map(lambda a: lax.all_gather(a, axis), part)

    def take(source):
        return jax.tree.map(lambda a: lax.dynamic_index_in_dim(a, source, 0, False), gathered)

    return lax.fori_loop(
        1, lax.axis_size(axis), lambda source, state: combine(state, take(source)), take(0)
    )


def combine(earlier, later):
    peak_early, sum_early, out_early = earlier
    peak_late, sum_late, out_late = later
    row_peak = jnp.maximum(peak_early, peak_late)
    factor_early = jnp.exp(peak_early - row_peak)
    factor_late = jnp.exp(peak_late - row_peak)
    weight_sum = sum_early * factor_early + sum_late * factor_late
    out_sum = out_early * factor_early[..., None] + out_late * factor_late[..., None]
    return (row_peak, weight_sum, out_sum)


def body(
    queries,
    key_pool,
    value_pool,
    block_table,
    lengths,
    residual_in,
    out_weight,
    norm_gain,
    gate_weight,
    up_weight,
    down_weight,
):
    requests = queries.shape[0]
    kv_local = key_pool.shape[2] // HD
    heads_local = queries.shape[1] // HD
    group_size = heads_local // kv_local
    blocks = block_table.shape[1] // requests
    shard_span = blocks * key_pool.shape[1]
    shard_index = lax.axis_index("kvp")
    page_ids = block_table[0].reshape(requests, blocks)
    key_rows = key_pool[page_ids].reshape(requests, shard_span, kv_local, HD)
    value_rows = value_pool[page_ids].reshape(requests, shard_span, kv_local, HD)
    query_heads = queries.reshape(requests, kv_local, group_size, HD)
    scores = jnp.einsum(
        "bkgd,btkd->bkgt", query_heads, key_rows, preferred_element_type=jnp.float32
    ) * HD ** (-0.5)
    positions = shard_index * shard_span + jnp.arange(shard_span, dtype=jnp.int32)
    is_live = (positions[None, :] < lengths[:, None])[:, None, None, :]
    masked = jnp.where(is_live, scores, -1e30)
    row_peak = jnp.max(masked, axis=-1)
    weights = jnp.where(is_live, jnp.exp(masked - row_peak[..., None]), 0.0)
    weight_sum = jnp.sum(weights, axis=-1).reshape(requests, heads_local)
    rounded = weights.astype(jnp.bfloat16)
    out_sum = jnp.einsum("bkgt,btkd->bkgd", rounded, value_rows, preferred_element_type=jnp.float32)
    out_sum = out_sum.reshape(requests, heads_local, HD)
    row_peak = row_peak.reshape(requests, heads_local)
    row_peak, weight_sum, out_sum = merged((row_peak, weight_sum, out_sum), "kvp", combine)
    attended = (
        (out_sum / weight_sum[..., None]).astype(jnp.bfloat16).reshape(requests, heads_local * HD)
    )
    projected = jnp.dot(attended, out_weight, preferred_element_type=jnp.float32)
    mixed = residual_in + lax.psum(projected, "tp")
    squares = lax.psum(jnp.sum(mixed * mixed, axis=1), "kvp")
    inv_rms = lax.rsqrt(squares / D + 0.1)
    normed = (mixed * inv_rms[:, None] * norm_gain.astype(jnp.float32)).astype(jnp.bfloat16)
    gate_part = jnp.dot(normed, gate_weight, preferred_element_type=jnp.float32)
    up_part = jnp.dot(normed, up_weight, preferred_element_type=jnp.float32)
    gate_full, up_full = lax.psum((gate_part, up_part), "kvp")
    hidden = (jax.nn.silu(gate_full) * up_full).astype(jnp.bfloat16)
    down_part = jnp.dot(hidden, down_weight, preferred_element_type=jnp.float32)
    layer_out = mixed + lax.psum(down_part, "tp")
    return (attended, layer_out)


def solution(mesh):
    return jax.shard_map(
        body,
        mesh=mesh,
        in_specs=(
            P(None, "tp"),
            P("kvp", None, "tp"),
            P("kvp", None, "tp"),
            P("kvp", None),
            P(),
            P(None, "kvp"),
            P("tp", "kvp"),
            P("kvp"),
            P("kvp", "tp"),
            P("kvp", "tp"),
            P("tp", "kvp"),
        ),
        out_specs=(P(None, "tp"), P(None, "kvp")),
        check_vma=False,
    )
```

profile of v0, /device:TPU:0, one launch (start us, length us, event | category | flops | bytes accessed | tf_op | source)
XLA Modules:
  0.0 310.6 jit_solution(2432256013141088473)
XLA Ops:
  7.8 1.4 reduce.3
  9.3 2.0 gather_fusion
  11.3 4.0 %reshape.77 = bf16[8,256,4,128]{3,2,1,0:T(4,128)(2,1)} reshape(bf16[32,64,512]{2,1,0:T(8,128)(2,1)} %gather_fusion) | data formatting | bytes 4194304 | tf_op jit(solution)/shard_map/reshape | solution.py:53
  15.3 3.6 %gather_fusion.1 = bf16[32,64,512]{2,1,0:T(8,128)(2,1)} fusion(bf16[32,64,512]{2,1,0:T(8,128)(2,1)} %param.15, s32[1024]{0:T(1024)S(1)} %pad_clamp_fusion), kind=kCustom, calls=%fused_computation.1 | custom fusion | bytes 4194432 | tf_op jit(solution)/shard_map/gather | solution.py:54
  18.9 4.0 %reshape.79 = bf16[8,256,4,128]{3,2,1,0:T(4,128)(2,1)} reshape(bf16[32,64,512]{2,1,0:T(8,128)(2,1)} %gather_fusion.1) | data formatting | bytes 4194304 | tf_op jit(solution)/shard_map/reshape | solution.py:54
  23.0 2.5 fusion.34
  25.4 1.1 fusion.16
  27.0 42.8 %all_gather.10 = f32[16,8,32]{2,1,0:T(8,128)S(1)} all-gather(f32[1,8,32]{2,1,0:T(8,128)S(1)} %all_gather_reshape.10), channel_id=1, replica_groups=mesh['kvp'=16,'tp'=2] {'kvp'}, dimensions={0}, use_global_device_ids=true | all-gather | bytes 17408 | tf_op jit(solution)/shard_map/all_gather | solution.py:11
  69.8 36.0 %all_gather.9 = f32[16,8,32]{2,1,0:T(8,128)S(1)} all-gather(f32[1,8,32]{2,1,0:T(8,128)S(1)} %all_gather_reshape.9), channel_id=1, replica_groups=mesh['kvp'=16,'tp'=2] {'kvp'}, dimensions={0}, use_global_device_ids=true | all-gather | bytes 17408 | tf_op jit(solution)/shard_map/all_gather | solution.py:11
  106.8 16.8 %while.19 = (s32[]{:T(128)}, f32[8,32]{1,0:T(8,128)S(1)}, f32[8,32]{1,0:T(8,128)S(1)}, f32[8,32,128]{2,1,0:T(8,128)S(1)}, f32[16,8,32]{2,1,0:T(8,128)S(1)}, /*in...) while((s32[]{:T(128)}, f32[8,32]{1,0:T(8,128)S(1)}, ...), condition=%wide.region_3.4_spmd, body=%wide.region_2.3_spmd.sunk | while | flops 99845 | bytes 403607 | solution.py:16
  106.8 1.1 fusion.44
  107.9 1.1 fusion.44
  110.2 1.1 fusion.44
  111.3 1.1 fusion.44
  113.5 1.1 fusion.44
  115.8 1.1 fusion.44
  123.7 2.9 fusion.35
  126.6 3.4 %psum.35 = f32[8,512]{1,0:T(8,128)S(1)} all-reduce(f32[8,512]{1,0:T(8,128)S(1)} %fusion.35), channel_id=1, replica_groups=mesh['kvp'=16,'tp'=2] {'tp'}, use_global_device_ids=true, to_apply=%region_4.5 | all-reduce | flops 4096 | bytes 32768 | tf_op jit(solution)/shard_map/psum | solution.py:74
  130.1 38.6 %psum.36 = f32[8]{0:T(128)S(1)} all-reduce(f32[8]{0:T(128)S(1)} %get-tuple-element.201), channel_id=1, replica_groups=mesh['kvp'=16,'tp'=2] {'kvp'}, use_global_device_ids=true, to_apply=%region_6.7 | all-reduce | flops 8 | bytes 64 | tf_op jit(solution)/shard_map/psum | solution.py:75
  168.7 8.0 %fusion.32 = f32[8,14336]{1,0:T(8,128)} fusion(bf16[512,14336]{1,0:T(8,128)(2,1)} %param.21, f32[8,512]{1,0:T(8,128)S(1)} %get-tuple-element.202, f32[512]{0:T(512)S(1)} %convert_element_type.17, f32[8]{0:T(128)S(1)} %add_rsqrt_fusion), kind=kOutput, calls=%fused_computation.44 | convolution fusion | flops 117452800 | bytes 15157280 | tf_op jit(solution)/shard_map/dot_general | solution.py:78
  176.8 8.0 %fusion.31 = f32[8,14336]{1,0:T(8,128)} fusion(bf16[512,14336]{1,0:T(8,128)(2,1)} %param.22, f32[8,512]{1,0:T(8,128)S(1)} %get-tuple-element.202, f32[512]{0:T(512)S(1)} %convert_element_type.17, f32[8]{0:T(128)S(1)} %add_rsqrt_fusion), kind=kOutput, calls=%fused_computation.43 | convolution fusion | flops 117452800 | bytes 15157280 | tf_op jit(solution)/shard_map/dot_general | solution.py:79
  184.8 107.5 %all-reduce.3.cloned.1.call-done = (f32[8,14336]{1,0:T(8,128)}, f32[8,14336]{1,0:T(8,128)}) async-done(((f32[8,14336]{1,0:T(8,128)}, f32[8,14336]{1,0:T(8,128)}), (f32[8,14336]{1,0:T(8,128)}, f32[8,14336]{1,0:T(8,128)})) %all-reduce.3.cloned.1.call-update) | async-done | bytes 917520 | tf_op jit(solution)/shard_map/psum | solution.py:80
  292.3 7.5 %fusion.19 = f32[8,512]{1,0:T(8,128)S(1)} fusion(bf16[14336,512]{1,0:T(8,128)(2,1)} %param.23, f32[8,14336]{1,0:T(8,128)} %get-tuple-element.195, f32[8,14336]{1,0:T(8,128)} %get-tuple-element.196), kind=kOutput, calls=%fused_computation.20 | convolution fusion | flops 118128640 | bytes 15613952 | tf_op jit(solution)/shard_map/dot_general | solution.py:82
  299.8 3.4 %psum.39 = f32[8,512]{1,0:T(8,128)S(1)} all-reduce(f32[8,512]{1,0:T(8,128)S(1)} %fusion.19), channel_id=1, replica_groups=mesh['kvp'=16,'tp'=2] {'tp'}, use_global_device_ids=true, to_apply=%region_9.10 | all-reduce | flops 4096 | bytes 32768 | tf_op jit(solution)/shard_map/psum | solution.py:83
  (62 shorter events, 13.0 us)
Async XLA Ops:
  7.2 2.1 copy-start
  7.2 98.7 %all-gather.2.cloned.1.call-start = ((), (), s32[]{:S(2)}) async-start(), calls=%async_computation | async-start | bytes 2228224 | tf_op jit(solution)/shard_map/all_gather | solution.py:11
  18.9 4.0 %copy-start.5 = (s32[8]{0:T(128)S(1)}, s32[8]{0:T(128)}, u32[]{:S(2)}) copy-start(s32[8]{0:T(128)} %param.17) | copy-start | bytes 100
  18.9 4.1 %copy-start.6 = (bf16[8,4096]{1,0:T(8,128)(2,1)S(1)}, bf16[8,4096]{1,0:T(8,128)(2,1)}, u32[]{:S(2)}) copy-start(bf16[8,4096]{1,0:T(8,128)(2,1)} %param.13) | copy-start | bytes 196612
  22.9 2.5 copy-start.1
  25.4 1.6 copy-start.4
  26.6 265.7 %all-reduce.3.cloned.1.call-start = ((), (), s32[]{:S(2)}) async-start(), calls=%async_computation.1 | async-start | bytes 1835008 | tf_op jit(solution)/shard_map/psum | solution.py:80
  123.7 2.9 copy-start.2
  123.7 6.2 %copy-start.3 = (f32[8,512]{1,0:T(8,128)S(1)}, f32[8,512]{1,0:T(8,128)}, u32[]{:S(2)}) copy-start(f32[8,512]{1,0:T(8,128)} %param.18) | copy-start | bytes 49156
Sparse Core Ops, SparseCore 0:
  26.7 63.5 all-gather.1
  184.9 107.3 all-reduce.2
where the time goes:
time: 311 us
  blocking collectives  124 us (40%)
  waiting for transfers between devices  108 us (35%)
  matrix products  29.9 us (10%)
  other arithmetic  18.9 us (6%)
  local copies, waits for them, and re-layouts  15.4 us (5%)
  between operations  14.1 us (5%)
    psum x1, waiting for transfers between devices, body(): gate_full, up_full = lax.psum((gate_part, up_part), 'kvp')  108 us
    all_gather x2, blocking collectives, merged(): gathered = jax.tree.map(lambda a: lax.all_gather(a, axis), part)  78.9 us
    psum x1, blocking collectives, body(): squares = lax.psum(jnp.sum(mixed * mixed, axis=1), 'kvp')  38.6 us
    add x15, other arithmetic, combine(): out_early * factor_early[..., None] + out_late * factor_late[..., None]  16.1 us
    dot_general x1, matrix products, body(): gate_part = jnp.dot(normed, gate_weight, preferred_element_type=jnp.float32)  8.02 us
    dot_general x1, matrix products, body(): up_part = jnp.dot(normed, up_weight, preferred_element_type=jnp.float32)  7.99 us
    dot_general x1, matrix products, body(): down_part = jnp.dot(hidden, down_weight, preferred_element_type=jnp.float32)  7.46 us
  transfers between devices with their start and end apart: 2, of which 1 were waited for; matrix products, arithmetic and copies ran while one was open for 0% of the time, Pallas kernels for 0%

commit v1 on v0

--- a/solution.py
+++ b/solution.py
@@ -72,7 +72,7 @@
     )
     projected = jnp.dot(attended, out_weight, preferred_element_type=jnp.float32)
     mixed = residual_in + lax.psum(projected, "tp")
-    squares = lax.psum(jnp.sum(mixed * mixed, axis=1), "kvp")
+    squares = jnp.sum(lax.all_gather(jnp.sum(mixed * mixed, axis=1), "kvp"), axis=0)
     inv_rms = lax.rsqrt(squares / D + 0.1)
     normed = (mixed * inv_rms[:, None] * norm_gain.astype(jnp.float32)).astype(jnp.bfloat16)
     gate_part = jnp.dot(normed, gate_weight, preferred_element_type=jnp.float32)

time: 311 us -> 313 us (level)
    psum x1 -> x0, blocking collectives: 38.6 us -> none  [body(): squares = lax.psum(jnp.sum(mixed * mixed, axis=1), 'kvp')]
    unnamed x0 -> x1, blocking collectives: none -> 38.2 us
where the time goes in v1:
time: 313 us; the launch traced here: 312 us
  blocking collectives  124 us (40%)
  waiting for transfers between devices  108 us (35%)
  matrix products  29.9 us (10%)
  other arithmetic  18.9 us (6%)
  local copies, waits for them, and re-layouts  16.3 us (5%)
  between operations  14.8 us (5%)
    psum x1, waiting for transfers between devices, body(): gate_full, up_full = lax.psum((gate_part, up_part), 'kvp')  108 us
    all_gather x2, blocking collectives, merged(): gathered = jax.tree.map(lambda a: lax.all_gather(a, axis), part)  79.1 us
    unnamed x1, blocking collectives  38.2 us
    add x15, other arithmetic, combine(): out_early * factor_early[..., None] + out_late * factor_late[..., None]  16.1 us
    dot_general x1, matrix products, body(): gate_part = jnp.dot(normed, gate_weight, preferred_element_type=jnp.float32)  8.03 us
    dot_general x1, matrix products, body(): up_part = jnp.dot(normed, up_weight, preferred_element_type=jnp.float32)  7.99 us
    dot_general x1, matrix products, body(): down_part = jnp.dot(hidden, down_weight, preferred_element_type=jnp.float32)  7.46 us
  transfers between devices with their start and end apart: 2, of which 1 were waited for; matrix products, arithmetic and copies ran while one was open for 0% of the time, Pallas kernels for 0%

profile of v1, /device:TPU:0, one launch (start us, length us, event | category | flops | bytes accessed | tf_op | source)
XLA Modules:
  0.0 312.3 jit_solution(6411887890923350178)
XLA Ops:
  7.8 1.4 reduce.3
  9.3 2.0 gather_fusion
  11.3 4.0 %reshape.81 = bf16[8,256,4,128]{3,2,1,0:T(4,128)(2,1)} reshape(bf16[32,64,512]{2,1,0:T(8,128)(2,1)} %gather_fusion) | data formatting | bytes 4194304 | tf_op jit(solution)/shard_map/reshape | solution.py:53
  15.3 3.6 %gather_fusion.1 = bf16[32,64,512]{2,1,0:T(8,128)(2,1)} fusion(bf16[32,64,512]{2,1,0:T(8,128)(2,1)} %param.15, s32[1024]{0:T(1024)S(1)} %pad_clamp_fusion), kind=kCustom, calls=%fused_computation.1 | custom fusion | bytes 4194432 | tf_op jit(solution)/shard_map/gather | solution.py:54
  18.9 4.0 %reshape.83 = bf16[8,256,4,128]{3,2,1,0:T(4,128)(2,1)} reshape(bf16[32,64,512]{2,1,0:T(8,128)(2,1)} %gather_fusion.1) | data formatting | bytes 4194304 | tf_op jit(solution)/shard_map/reshape | solution.py:54
  23.0 2.5 fusion.34
  25.4 1.1 fusion.16
  28.3 42.8 %all_gather.16 = f32[16,8,32]{2,1,0:T(8,128)S(1)} all-gather(f32[1,8,32]{2,1,0:T(8,128)S(1)} %all_gather_reshape.10), channel_id=1, replica_groups=mesh['kvp'=16,'tp'=2] {'kvp'}, dimensions={0}, use_global_device_ids=true | all-gather | bytes 17408 | tf_op jit(solution)/shard_map/all_gather | solution.py:11
  71.1 36.3 %all_gather.15 = f32[16,8,32]{2,1,0:T(8,128)S(1)} all-gather(f32[1,8,32]{2,1,0:T(8,128)S(1)} %all_gather_reshape.9), channel_id=1, replica_groups=mesh['kvp'=16,'tp'=2] {'kvp'}, dimensions={0}, use_global_device_ids=true | all-gather | bytes 17408 | tf_op jit(solution)/shard_map/all_gather | solution.py:11
  108.3 16.8 %while.19 = (s32[]{:T(128)}, f32[8,32]{1,0:T(8,128)S(1)}, f32[8,32]{1,0:T(8,128)S(1)}, f32[8,32,128]{2,1,0:T(8,128)S(1)}, f32[16,8,32]{2,1,0:T(8,128)S(1)}, /*in...) while((s32[]{:T(128)}, f32[8,32]{1,0:T(8,128)S(1)}, ...), condition=%wide.region_3.4_spmd, body=%wide.region_2.3_spmd.sunk | while | flops 99845 | bytes 403607 | solution.py:16
  108.4 1.1 fusion.44
  110.6 1.1 fusion.44
  114.0 1.1 fusion.44
  116.2 1.1 fusion.44
  117.3 1.1 fusion.44
  119.6 1.1 fusion.44
  125.3 2.9 fusion.35
  128.1 3.4 %psum.28 = f32[8,512]{1,0:T(8,128)S(1)} all-reduce(f32[8,512]{1,0:T(8,128)S(1)} %fusion.35), channel_id=1, replica_groups=mesh['kvp'=16,'tp'=2] {'tp'}, use_global_device_ids=true, to_apply=%region_4.5 | all-reduce | flops 4096 | bytes 32768 | tf_op jit(solution)/shard_map/psum | solution.py:74
  131.9 38.2 %all-reduce = f32[128]{0:T(128)S(1)} all-reduce(f32[128]{0:T(128)S(1)} %dynamic-update-slice), channel_id=2, replica_groups=mesh['kvp'=16,'tp'=2] {'kvp'}, use_global_device_ids=true, to_apply=%add | all-reduce | flops 128 | bytes 1024
  170.2 8.0 %fusion.32 = f32[8,14336]{1,0:T(8,128)} fusion(bf16[512,14336]{1,0:T(8,128)(2,1)} %param.21, f32[8,512]{1,0:T(8,128)S(1)} %get-tuple-element.202, f32[512]{0:T(512)S(1)} %convert_element_type.17, f32[8]{0:T(128)S(1)} %add_rsqrt_fusion), kind=kOutput, calls=%fused_computation.44 | convolution fusion | flops 117452800 | bytes 15157280 | tf_op jit(solution)/shard_map/dot_general | solution.py:78
  178.2 8.0 %fusion.31 = f32[8,14336]{1,0:T(8,128)} fusion(bf16[512,14336]{1,0:T(8,128)(2,1)} %param.22, f32[8,512]{1,0:T(8,128)S(1)} %get-tuple-element.202, f32[512]{0:T(512)S(1)} %convert_element_type.17, f32[8]{0:T(128)S(1)} %add_rsqrt_fusion), kind=kOutput, calls=%fused_computation.43 | convolution fusion | flops 117452800 | bytes 15157280 | tf_op jit(solution)/shard_map/dot_general | solution.py:79
  186.3 107.8 %all-reduce.4.cloned.1.call-done = (f32[8,14336]{1,0:T(8,128)}, f32[8,14336]{1,0:T(8,128)}) async-done(((f32[8,14336]{1,0:T(8,128)}, f32[8,14336]{1,0:T(8,128)}), (f32[8,14336]{1,0:T(8,128)}, f32[8,14336]{1,0:T(8,128)})) %all-reduce.4.cloned.1.call-update) | async-done | bytes 917520 | tf_op jit(solution)/shard_map/psum | solution.py:80
  294.0 7.5 %fusion.19 = f32[8,512]{1,0:T(8,128)S(1)} fusion(bf16[14336,512]{1,0:T(8,128)(2,1)} %param.23, f32[8,14336]{1,0:T(8,128)} %get-tuple-element.195, f32[8,14336]{1,0:T(8,128)} %get-tuple-element.196), kind=kOutput, calls=%fused_computation.20 | convolution fusion | flops 118128640 | bytes 15613952 | tf_op jit(solution)/shard_map/dot_general | solution.py:82
  301.5 3.4 %psum.31 = f32[8,512]{1,0:T(8,128)S(1)} all-reduce(f32[8,512]{1,0:T(8,128)S(1)} %fusion.19), channel_id=1, replica_groups=mesh['kvp'=16,'tp'=2] {'tp'}, use_global_device_ids=true, to_apply=%region_9.10 | all-reduce | flops 4096 | bytes 32768 | tf_op jit(solution)/shard_map/psum | solution.py:83
  (69 shorter events, 13.9 us)
Async XLA Ops:
  7.2 2.1 copy-start
  7.2 100.2 %all-gather.3.cloned.1.call-start = ((), (), s32[]{:S(2)}) async-start(), calls=%async_computation | async-start | bytes 2228224 | tf_op jit(solution)/shard_map/all_gather | solution.py:11
  18.9 4.0 %copy-start.5 = (s32[8]{0:T(128)S(1)}, s32[8]{0:T(128)}, u32[]{:S(2)}) copy-start(s32[8]{0:T(128)} %param.17) | copy-start | bytes 100
  18.9 4.1 %copy-start.6 = (bf16[8,4096]{1,0:T(8,128)(2,1)S(1)}, bf16[8,4096]{1,0:T(8,128)(2,1)}, u32[]{:S(2)}) copy-start(bf16[8,4096]{1,0:T(8,128)(2,1)} %param.13) | copy-start | bytes 196612
  22.9 2.6 copy-start.1
  25.4 1.6 copy-start.4
  25.4 1.6 copy-start.7
  26.6 267.5 %all-reduce.4.cloned.1.call-start = ((), (), s32[]{:S(2)}) async-start(), calls=%async_computation.1 | async-start | bytes 1835008 | tf_op jit(solution)/shard_map/psum | solution.py:80
  125.3 2.9 copy-start.2
  125.3 6.2 %copy-start.3 = (f32[8,512]{1,0:T(8,128)S(1)}, f32[8,512]{1,0:T(8,128)}, u32[]{:S(2)}) copy-start(f32[8,512]{1,0:T(8,128)} %param.18) | copy-start | bytes 49156
Sparse Core Ops, SparseCore 0:
  26.7 63.3 all-gather.2
  186.4 107.6 all-reduce.3
